TPU v7x, 512 devices: a whole 4x4x16 slice. The times are simulated.
512 devices in a mesh: dp: 128 (over y, x, z_hi, core), mp: 4 (over z_lo).
Axes of the slice: x: 4, y: 4, z: 16 (z_hi: 4, z_lo: 4; z = z_hi * 4 + z_lo), core: 2. Of those that a mesh axis runs over, the one named last changes fastest.
Arguments:
- layer_input: bfloat16 [512, 8192], P('dp'), may hold values from -6 to 6
- pre_act: bfloat16 [512, 8192], P('dp', 'mp'), may hold values from -8 to 8
- hidden_adjoint: bfloat16 [512, 8192], P('dp', 'mp'), may hold values from -6 to 6
- output_adjoint: bfloat16 [512, 8192], P('dp', 'mp'), may hold values from -6 to 6
Outputs:
- precond_in: float32 [8192, 8192], P('dp', 'mp')
- direction_in: float32 [8192, 8192], P('dp', 'mp')
- precond_out: float32 [8192, 8192], P('dp', 'mp')
- direction_out: float32 [8192, 8192], P('dp', 'mp')
- sq_norm: float32 [], replicated
All inputs are finite; a program needn't handle non-finite values.
Results may differ from a plain program's by a relative error of at most 0.0029.
Values may be sent and summed in bfloat16 or wider, within the bound.
A program may use at most 64 MiB of HBM per device.

v0:
```python
import jax
import jax.numpy as jnp
from jax import lax
from jax.sharding import Mesh
from jax.sharding import PartitionSpec as P

D = 8192
H = 8192
DP = ("dp_0", "dp_1", "dp_2", "dp_3")
DP_MP = ("dp_0", "dp_1", "dp_2", "dp_3", "mp")
DAMPING = 0.1
EXPONENT = 0.75


def in_order(pieces, dim):
    pieces = jnp.moveaxis(pieces, 0, dim)
    lengths = pieces.shape
    return pieces.reshape(*lengths[:dim], lengths[dim] * lengths[dim + 1], *lengths[dim + 2 :])


def copy_for_each(x, axis):
    size = lax.axis_size(axis)
    return lax.all_to_all(jnp.broadcast_to(x[None], (size, *x.shape)), axis, 0, 0, tiled=True)


def gather_directly(x, axis, dim):
    return in_order(copy_for_each(x, axis), dim)


def split_up(x, dim, size):
    before, after = (x.shape[:dim], x.shape[dim + 1 :])
    return jnp.moveaxis(x.reshape(*before, size, -1, *after), dim, 0)


def exchange_in_order(pieces, axes, turns):
    lengths = [lax.axis_size(a) for a in axes]
    pieces = pieces.reshape(*lengths, *pieces.shape[1:])
    for k in turns:
        pieces = lax.all_to_all(pieces, axes[k], split_axis=k, concat_axis=k, tiled=True)
    return pieces.reshape(-1, *pieces.shape[len(axes) :])


def two_step_exchange(x, groups, turns, split_dim, concat_dim):
    size = lax.axis_size(groups[0]) * lax.axis_size(groups[1])
    pieces = split_up(x, split_dim, size)
    return in_order(exchange_in_order(pieces, groups, turns), concat_dim)


def side_by_side(arrays, axis, dim, along):
    ends, at = ([], 0)
    for a in arrays[:-1]:
        at += a.shape[along]
        ends.append(at)
    both = jnp.concatenate(arrays, axis=along)
    return tuple(jnp.split(lax.all_gather(both, axis, axis=dim, tiled=True), ends, axis=along))


def over_axes(x, axes):
    for axis in axes:
        x = lax.psum(x, axis)
    return x


def square_bf(values):
    wide = values.astype(jnp.float32)
    return (wide * wide).astype(jnp.bfloat16)


def accumulate(act_block, sq_block, adj_piece):
    contract = (((0,), (0,)), ((), ()))
    grad_sum = lax.dot_general(act_block, adj_piece, contract, preferred_element_type=jnp.float32)
    square_sum = lax.dot_general(
        sq_block, square_bf(adj_piece), contract, preferred_element_type=jnp.float32
    )
    return (grad_sum, square_sum)


def finish(partial_value, total_rows):
    gradient = partial_value[0] / total_rows
    precond = (partial_value[1] / total_rows + DAMPING) ** EXPONENT
    norm_term = jnp.sum(gradient * gradient / precond)
    return (gradient, precond, norm_term)


def shards(layer_input, pre_act, hidden_adjoint, output_adjoint):
    preact = pre_act.astype(jnp.float32)
    logistic = jax.nn.sigmoid(preact)
    hidden = (preact * logistic).astype(jnp.bfloat16)
    adjoint = (
        hidden_adjoint.astype(jnp.float32) * logistic * (1.0 + preact * (1.0 - logistic))
    ).astype(jnp.bfloat16)
    own_input = lax.all_to_all(layer_input, DP, split_axis=1, concat_axis=0, tiled=True)
    sq_input = square_bf(own_input)
    total_rows = own_input.shape[0]
    wide_hidden = gather_directly(hidden, "mp", 1)
    own_hidden = two_step_exchange(wide_hidden, (("dp_0", "dp_1", "dp_2"), "dp_3"), (1, 0), 1, 0)
    sq_hidden = square_bf(own_hidden)
    pieces = side_by_side((adjoint, output_adjoint), DP, 0, 1)
    first_part = accumulate(own_input, sq_input, pieces[0])
    second_part = accumulate(own_hidden, sq_hidden, pieces[1])
    gradient_in, precond_in, term_in = finish(first_part, total_rows)
    gradient_out, precond_out, term_out = finish(second_part, total_rows)
    sq_norm = over_axes(term_in + term_out, DP_MP)
    rescale = jnp.sqrt(2.0 * D * H / sq_norm)
    direction_in = gradient_in / precond_in * rescale
    direction_out = gradient_out / precond_out * rescale
    return (precond_in, direction_in, precond_out, direction_out, sq_norm)


def solution(mesh):
    torus = Mesh(
        mesh.devices.reshape(4, 4, 4, 2, mesh.shape["mp"]), ("dp_0", "dp_1", "dp_2", "dp_3", "mp")
    )
    placed = (P(DP, None), P(DP, "mp"), P(DP, "mp"), P(DP, "mp"))
    return jax.shard_map(
        shards,
        mesh=torus,
        in_specs=placed,
        out_specs=(P(DP, "mp"), P(DP, "mp"), P(DP, "mp"), P(DP, "mp"), P()),
        check_vma=False,
    )
```

profile of v0, /device:TPU:32, one launch (start us, length us, event | category | flops | bytes accessed | tf_op | source)
XLA Modules:
  0.0 210.1 jit_solution(18236963314669672673)
XLA Ops:
  7.2 0.0 all-gather.3.cloned.1.call-start
  7.2 0.8 fusion.13
  8.0 1.3 maximum_bitcast_fusion
  9.3 0.0 all-gather.3.cloned.1.call-update
  9.4 0.6 broadcast_in_dim.2
  10.0 8.7 %all-to-all-start.1 = ((bf16[4,4,2048]{2,1,0:T(4,128)(2,1)}), bf16[4,4,2048]{2,1,0:T(4,128)(2,1)S(1)}, u32[]{:S(2)}, u32[]{:S(2)}) async-start(bf16[4,4,2048]{2,1,0:T(4,128)(2,1)} %broadcast_in_dim.2), calls=%async_computation.1 | async-start | bytes 131072 | tf_op jit(solution)/shard_map/all_to_all | solution.py:23
  18.7 1.0 all_to_all.23
  19.7 0.1 copy.22
  19.8 0.7 reshape.20
  20.6 2.8 %all-to-all-done.1 = bf16[4,4,2048]{2,1,0:T(4,128)(2,1)S(1)} async-done(((bf16[4,4,2048]{2,1,0:T(4,128)(2,1)}), bf16[4,4,2048]{2,1,0:T(4,128)(2,1)S(1)}, u32[]{:S(2)}, u32[]{:S(2)}) %all-to-all-start.1) | async-done | bytes 65568 | tf_op jit(solution)/shard_map/all_to_all | solution.py:23
  23.4 0.1 copy.16
  23.4 0.2 reshape_reshape.6
  23.6 0.1 copy.21
  23.7 0.2 reshape.22
  23.9 3.8 %all_to_all.34 = bf16[2,2,8192]{2,1,0:T(2,128)(2,1)S(1)} all-to-all(bf16[2,2,8192]{2,1,0:T(2,128)(2,1)S(1)} %reshape.22), channel_id=1, replica_groups=mesh['dp_0'=4,'dp_1'=4,'dp_2'=4,'dp_3'=2,'mp'=4] {'dp_3'}, dimensions={0} | all-to-all | bytes 131072 | tf_op jit(solution)/shard_map/all_to_all | solution.py:39
  27.7 17.1 %all-to-all-start = ((bf16[128,2,128]{2,1,0:T(2,128)(2,1)}), bf16[128,2,128]{2,1,0:T(2,128)(2,1)S(1)}, u32[]{:S(2)}, u32[]{:S(2)}) async-start(bf16[128,2,128]{2,1,0:T(2,128)(2,1)} %reshape.20), calls=%async_computation | async-start | bytes 131072 | tf_op jit(solution)/shard_map/all_to_all | solution.py:92
  44.7 0.1 reshape.23
  44.9 0.8 reshape.24
  45.7 16.7 %all-to-all-done = bf16[128,2,128]{2,1,0:T(2,128)(2,1)S(1)} async-done(((bf16[128,2,128]{2,1,0:T(2,128)(2,1)}), bf16[128,2,128]{2,1,0:T(2,128)(2,1)S(1)}, u32[]{:S(2)}, u32[]{:S(2)}) %all-to-all-start) | async-done | bytes 65568 | tf_op jit(solution)/shard_map/all_to_all | solution.py:92
  62.4 4.6 %all-to-all-start.3 = ((bf16[64,2,256]{2,1,0:T(2,128)(2,1)}), bf16[64,2,256]{2,1,0:T(2,128)(2,1)S(1)}, u32[]{:S(2)}, u32[]{:S(2)}) async-start(bf16[64,2,256]{2,1,0:T(2,128)(2,1)} %reshape.24), calls=%async_computation.3 | async-start | bytes 131072 | tf_op jit(solution)/shard_map/all_to_all | solution.py:39
  67.0 0.1 reshape.21
  67.1 18.8 %all-to-all-done.3 = bf16[64,2,256]{2,1,0:T(2,128)(2,1)S(1)} async-done(((bf16[64,2,256]{2,1,0:T(2,128)(2,1)}), bf16[64,2,256]{2,1,0:T(2,128)(2,1)S(1)}, u32[]{:S(2)}, u32[]{:S(2)}) %all-to-all-start.3) | async-done | bytes 65568 | tf_op jit(solution)/shard_map/all_to_all | solution.py:39
  85.9 0.1 reshape.25
  86.1 47.5 %all-gather.3.cloned.1.call-done = bf16[128,4,4096]{2,1,0:T(4,128)(2,1)} async-done(((bf16[1,4,4096]{2,1,0:T(4,128)(2,1)}), bf16[128,4,4096]{2,1,0:T(4,128)(2,1)}) %all-gather.3.cloned.1.call-update) | async-done | bytes 4194320 | tf_op jit(solution)/shard_map/all_gather | solution.py:55
  133.6 6.9 %reshape.19 = bf16[512,4096]{1,0:T(8,128)(2,1)} reshape(bf16[128,4,4096]{2,1,0:T(4,128)(2,1)} %all-gather.3.cloned.1.call-done) | data formatting | bytes 8388608
  140.5 0.0 copy-start
  140.5 2.3 %fusion = f32[64,2048]{1,0:T(8,128)S(1)} fusion(bf16[512,4096]{1,0:T(8,128)(2,1)} %reshape.19, bf16[512,64]{1,0:T(8,128)(2,1)S(1)} %bitcast.29), kind=kOutput, calls=%fused_computation.6 | convolution fusion | flops 137723904 | bytes 2686976 | tf_op jit(solution)/shard_map/dot_general | solution.py:72
  142.8 2.9 %multiply_reduce_fusion.1 = (f32[]{:T(128)}, f32[64,2048]{1,0:T(8,128)S(1)}) fusion(f32[64,2048]{1,0:T(8,128)S(1)} %fusion, bf16[512,64]{1,0:T(8,128)(2,1)S(1)} %bitcast.30, bf16[512,4096]{1,0:T(8,128)(2,1)} %reshape.19), kind=kOutput, calls=%fused_computation.15 | convolution fusion | flops 134742016 | bytes 3211268 | tf_op jit(solution)/shard_map/dot_general | solution.py:71
  145.7 0.0 copy-done
  145.7 0.6 fusion.2
  146.3 1.2 multiply_reduce_fusion
  148.8 11.3 %psum.35 = f32[]{:T(128)} all-reduce(f32[]{:T(128)S(6)} %add.29), channel_id=1, replica_groups=mesh['dp_0'=4,'dp_1'=4,'dp_2'=4,'dp_3'=2,'mp'=4] {'dp_0'}, use_global_device_ids=true, to_apply=%region_2.0 | all-reduce | flops 1 | bytes 8 | tf_op jit(solution)/shard_map/psum | solution.py:60
  160.1 11.0 %psum.36 = f32[]{:T(128)} all-reduce(f32[]{:T(128)} %psum.35), channel_id=1, replica_groups=mesh['dp_0'=4,'dp_1'=4,'dp_2'=4,'dp_3'=2,'mp'=4] {'dp_1'}, use_global_device_ids=true, to_apply=%region_3.0 | all-reduce | flops 1 | bytes 8 | tf_op jit(solution)/shard_map/psum | solution.py:60
  171.2 14.1 %psum.37 = f32[]{:T(128)} all-reduce(f32[]{:T(128)} %psum.36), channel_id=1, replica_groups=mesh['dp_0'=4,'dp_1'=4,'dp_2'=4,'dp_3'=2,'mp'=4] {'dp_2'}, use_global_device_ids=true, to_apply=%region_4.0 | all-reduce | flops 1 | bytes 8 | tf_op jit(solution)/shard_map/psum | solution.py:60
  185.3 3.1 %psum.38 = f32[]{:T(128)} all-reduce(f32[]{:T(128)} %psum.37), channel_id=1, replica_groups=mesh['dp_0'=4,'dp_1'=4,'dp_2'=4,'dp_3'=2,'mp'=4] {'dp_3'}, use_global_device_ids=true, to_apply=%region_5.0 | all-reduce | flops 1 | bytes 8 | tf_op jit(solution)/shard_map/psum | solution.py:60
  188.3 12.2 %psum.39 = f32[]{:T(128)} all-reduce(f32[]{:T(128)} %psum.38), channel_id=1, replica_groups=mesh['dp_0'=4,'dp_1'=4,'dp_2'=4,'dp_3'=2,'mp'=4] {'mp'}, use_global_device_ids=true, to_apply=%region_6.0 | all-reduce | flops 1 | bytes 8 | tf_op jit(solution)/shard_map/psum | solution.py:60
  201.3 2.0 multiply_multiply_fusion
  (1 shorter events, 0.0 us)
Async XLA Ops:
  7.2 126.4 %all-gather.3.cloned.1.call-start = ((), (), s32[]{:S(2)}) async-start(), calls=%async_computation.4 | async-start | bytes 4227072 | tf_op jit(solution)/shard_map/all_gather | solution.py:55
  10.0 13.3 %all-to-all-start.1 = ((bf16[4,4,2048]{2,1,0:T(4,128)(2,1)}), bf16[4,4,2048]{2,1,0:T(4,128)(2,1)S(1)}, u32[]{:S(2)}, u32[]{:S(2)}) async-start(bf16[4,4,2048]{2,1,0:T(4,128)(2,1)} %broadcast_in_dim.2), calls=%async_computation.1 | async-start | bytes 131072 | tf_op jit(solution)/shard_map/all_to_all | solution.py:23
  27.7 34.7 %all-to-all-start = ((bf16[128,2,128]{2,1,0:T(2,128)(2,1)}), bf16[128,2,128]{2,1,0:T(2,128)(2,1)S(1)}, u32[]{:S(2)}, u32[]{:S(2)}) async-start(bf16[128,2,128]{2,1,0:T(2,128)(2,1)} %reshape.20), calls=%async_computation | async-start | bytes 131072 | tf_op jit(solution)/shard_map/all_to_all | solution.py:92
  62.4 23.5 %all-to-all-start.3 = ((bf16[64,2,256]{2,1,0:T(2,128)(2,1)}), bf16[64,2,256]{2,1,0:T(2,128)(2,1)S(1)}, u32[]{:S(2)}, u32[]{:S(2)}) async-start(bf16[64,2,256]{2,1,0:T(2,128)(2,1)} %reshape.24), calls=%async_computation.3 | async-start | bytes 131072 | tf_op jit(solution)/shard_map/all_to_all | solution.py:39
  140.5 5.2 %copy-start = (bf16[512,4096]{1,0:T(8,128)(2,1)S(1)}, bf16[512,4096]{1,0:T(8,128)(2,1)}, u32[]{:S(2)}) copy-start(bf16[512,4096]{1,0:T(8,128)(2,1)} %reshape.19) | copy-start | bytes 12582916
Sparse Core Ops, SparseCore 0:
  13.0 120.5 all-gather.2
where the time goes:
time: 211 us; the launch traced here: 210 us
  waiting for transfers between devices  85.8 us (41%)
  blocking collectives  55.5 us (26%)
  starting transfers between devices  30.4 us (14%)
  between operations  16.1 us (8%)
  local copies, waits for them, and re-layouts  11.1 us (5%)
  matrix products  7.01 us (3%)
  other arithmetic  4.16 us (2%)
    psum x5, blocking collectives, over_axes(): x = lax.psum(x, axis)  51.7 us
    all_gather x1, waiting for transfers between devices, side_by_side(): lax.all_gather(both, axis, axis=dim, tiled=True)  47.5 us
    all_to_all x1, waiting for transfers between devices, exchange_in_order(): lax.all_to_all(pieces, axes[k], split_axis=k, concat_axis=k, tiled=True)  18.8 us
    all_to_all x1, starting transfers between devices, shards(): lax.all_to_all(layer_input, DP, split_axis=1, concat_axis=0, tiled=True)  17.1 us
    all_to_all x1, waiting for transfers between devices, shards(): lax.all_to_all(layer_input, DP, split_axis=1, concat_axis=0, tiled=True)  16.7 us
    unnamed x9, local copies, waits for them, and re-layouts  8.99 us
    all_to_all x1, starting transfers between devices, copy_for_each(): lax.all_to_all(jnp.broadcast_to(x[None], (size, *x.shape)), axis, 0, 0, t...  8.71 us
    all_to_all x1, starting transfers between devices, exchange_in_order(): lax.all_to_all(pieces, axes[k], split_axis=k, concat_axis=k, tiled=True)  4.62 us
  transfers between devices with their start and end apart: 4, of which 4 were waited for; matrix products, arithmetic and copies ran while one was open for 2% of the time, Pallas kernels for 0%

commit v1 on v0

--- a/solution.py
+++ b/solution.py
@@ -57,7 +57,7 @@
 
 def over_axes(x, axes):
     for axis in axes:
-        x = lax.psum(x, axis)
+        x = jnp.sum(lax.all_gather(x, axis), axis=0)
     return x
 
 

time: 211 us -> 222 us (1.052)
  local copies, waits for them, and re-layouts: 11.1 us -> 23.8 us
  blocking collectives: 55.5 us -> 52.4 us
  other arithmetic: 4.16 us -> 7.18 us
    psum x5 -> x0, blocking collectives: 51.7 us -> none  [over_axes(): x = lax.psum(x, axis)]
    unnamed x0 -> x5, blocking collectives: none -> 48.6 us
    unnamed x9 -> x24, local copies, waits for them, and re-layouts: 8.99 us -> 21.7 us
    reduce_sum x0 -> x5, other arithmetic: none -> 3.02 us  [over_axes(): x = jnp.sum(lax.all_gather(x, axis), axis=0)]
where the time goes in v1:
time: 222 us; the launch traced here: 221 us
  waiting for transfers between devices  84.5 us (38%)
  blocking collectives  52.4 us (24%)
  starting transfers between devices  30.4 us (14%)
  local copies, waits for them, and re-layouts  23.8 us (11%)
  between operations  16.2 us (7%)
  other arithmetic  7.18 us (3%)
  matrix products  7.02 us (3%)
    unnamed x5, blocking collectives  48.6 us
    all_gather x1, waiting for transfers between devices, side_by_side(): lax.all_gather(both, axis, axis=dim, tiled=True)  47.5 us
    unnamed x24, local copies, waits for them, and re-layouts  21.7 us
    all_to_all x1, waiting for transfers between devices, exchange_in_order(): lax.all_to_all(pieces, axes[k], split_axis=k, concat_axis=k, tiled=True)  17.5 us
    all_to_all x1, starting transfers between devices, shards(): lax.all_to_all(layer_input, DP, split_axis=1, concat_axis=0, tiled=True)  17.1 us
    all_to_all x1, waiting for transfers between devices, shards(): lax.all_to_all(layer_input, DP, split_axis=1, concat_axis=0, tiled=True)  16.7 us
    all_to_all x1, starting transfers between devices, copy_for_each(): lax.all_to_all(jnp.broadcast_to(x[None], (size, *x.shape)), axis, 0, 0, t...  8.71 us
    all_to_all x1, starting transfers between devices, exchange_in_order(): lax.all_to_all(pieces, axes[k], split_axis=k, concat_axis=k, tiled=True)  4.62 us
  transfers between devices with their start and end apart: 4, of which 4 were waited for; matrix products, arithmetic and copies ran while one was open for 2% of the time, Pallas kernels for 0%

profile of v1, /device:TPU:32, one launch (start us, length us, event | category | flops | bytes accessed | tf_op | source)
XLA Modules:
  0.0 221.5 jit_solution(8277706337043241596)
XLA Ops:
  7.2 0.8 fusion.13
  8.0 1.3 maximum_bitcast_fusion
  9.4 0.6 broadcast_in_dim.2
  10.0 8.7 %all-to-all-start.1 = ((bf16[4,4,2048]{2,1,0:T(4,128)(2,1)}), bf16[4,4,2048]{2,1,0:T(4,128)(2,1)S(1)}, u32[]{:S(2)}, u32[]{:S(2)}) async-start(bf16[4,4,2048]{2,1,0:T(4,128)(2,1)} %broadcast_in_dim.2), calls=%async_computation.1 | async-start | bytes 131072 | tf_op jit(solution)/shard_map/all_to_all | solution.py:23
  18.7 1.0 all_to_all.23
  19.7 0.1 copy.22
  19.8 0.7 reshape.45
  20.6 2.8 %all-to-all-done.1 = bf16[4,4,2048]{2,1,0:T(4,128)(2,1)S(1)} async-done(((bf16[4,4,2048]{2,1,0:T(4,128)(2,1)}), bf16[4,4,2048]{2,1,0:T(4,128)(2,1)S(1)}, u32[]{:S(2)}, u32[]{:S(2)}) %all-to-all-start.1) | async-done | bytes 65568 | tf_op jit(solution)/shard_map/all_to_all | solution.py:23
  23.4 0.1 copy.16
  23.4 0.2 reshape_reshape.6
  23.6 0.1 copy.21
  23.7 0.2 reshape.47
  23.9 3.8 %all_to_all.34 = bf16[2,2,8192]{2,1,0:T(2,128)(2,1)S(1)} all-to-all(bf16[2,2,8192]{2,1,0:T(2,128)(2,1)S(1)} %reshape.47), channel_id=1, replica_groups=mesh['dp_0'=4,'dp_1'=4,'dp_2'=4,'dp_3'=2,'mp'=4] {'dp_3'}, dimensions={0} | all-to-all | bytes 131072 | tf_op jit(solution)/shard_map/all_to_all | solution.py:39
  27.7 17.1 %all-to-all-start = ((bf16[128,2,128]{2,1,0:T(2,128)(2,1)}), bf16[128,2,128]{2,1,0:T(2,128)(2,1)S(1)}, u32[]{:S(2)}, u32[]{:S(2)}) async-start(bf16[128,2,128]{2,1,0:T(2,128)(2,1)} %reshape.45), calls=%async_computation | async-start | bytes 131072 | tf_op jit(solution)/shard_map/all_to_all | solution.py:92
  44.7 0.1 reshape.48
  44.9 0.8 reshape.49
  45.7 16.7 %all-to-all-done = bf16[128,2,128]{2,1,0:T(2,128)(2,1)S(1)} async-done(((bf16[128,2,128]{2,1,0:T(2,128)(2,1)}), bf16[128,2,128]{2,1,0:T(2,128)(2,1)S(1)}, u32[]{:S(2)}, u32[]{:S(2)}) %all-to-all-start) | async-done | bytes 65568 | tf_op jit(solution)/shard_map/all_to_all | solution.py:92
  62.4 4.6 %all-to-all-start.3 = ((bf16[64,2,256]{2,1,0:T(2,128)(2,1)}), bf16[64,2,256]{2,1,0:T(2,128)(2,1)S(1)}, u32[]{:S(2)}, u32[]{:S(2)}) async-start(bf16[64,2,256]{2,1,0:T(2,128)(2,1)} %reshape.49), calls=%async_computation.3 | async-start | bytes 131072 | tf_op jit(solution)/shard_map/all_to_all | solution.py:39
  67.0 1.3 dynamic-slice
  68.3 0.1 reshape.46
  68.4 17.5 %all-to-all-done.3 = bf16[64,2,256]{2,1,0:T(2,128)(2,1)S(1)} async-done(((bf16[64,2,256]{2,1,0:T(2,128)(2,1)}), bf16[64,2,256]{2,1,0:T(2,128)(2,1)S(1)}, u32[]{:S(2)}, u32[]{:S(2)}) %all-to-all-start.3) | async-done | bytes 65568 | tf_op jit(solution)/shard_map/all_to_all | solution.py:39
  85.9 0.1 reshape.50
  86.1 47.5 %all-gather.3.cloned.1.call-done = bf16[128,4,4096]{2,1,0:T(4,128)(2,1)} async-done(((bf16[1,4,4096]{2,1,0:T(4,128)(2,1)}), bf16[128,4,4096]{2,1,0:T(4,128)(2,1)}) %all-gather.3.cloned.1.call-update) | async-done | bytes 4194320 | tf_op jit(solution)/shard_map/all_gather | solution.py:55
  133.6 6.9 %reshape.34 = bf16[512,4096]{1,0:T(8,128)(2,1)} reshape(bf16[128,4,4096]{2,1,0:T(4,128)(2,1)} %all-gather.3.cloned.1.call-done) | data formatting | bytes 8388608
  140.5 2.3 %fusion.2 = f32[64,2048]{1,0:T(8,128)S(1)} fusion(bf16[512,4096]{1,0:T(8,128)(2,1)} %reshape.34, bf16[512,64]{1,0:T(8,128)(2,1)S(1)} %bitcast.32), kind=kOutput, calls=%fused_computation.8 | convolution fusion | flops 137723904 | bytes 2686976 | tf_op jit(solution)/shard_map/dot_general | solution.py:72
  142.8 2.8 %multiply_reduce_fusion = (f32[]{:T(128)}, f32[64,2048]{1,0:T(8,128)S(1)}) fusion(f32[64,2048]{1,0:T(8,128)S(1)} %fusion.2, bf16[512,64]{1,0:T(8,128)(2,1)S(1)} %bitcast.33, bf16[512,4096]{1,0:T(8,128)(2,1)} %reshape.34), kind=kOutput, calls=%fused_computation.14 | convolution fusion | flops 134742016 | bytes 3211268 | tf_op jit(solution)/shard_map/dot_general | solution.py:71
  145.7 0.6 fusion
  146.2 1.3 multiply_reduce_fusion.1
  148.8 0.8 dynamic-update-slice
  149.6 1.3 dynamic-slice.1
  150.8 10.8 %all-reduce = f32[4]{0:T(128)S(1)} all-reduce(f32[4]{0:T(128)S(1)} %dynamic-update-slice), channel_id=1, replica_groups=mesh['dp_0'=4,'dp_1'=4,'dp_2'=4,'dp_3'=2,'mp'=4] {'dp_0'}, use_global_device_ids=true, to_apply=%add | all-reduce | flops 4 | bytes 32
  161.6 0.6 reduce_sum.65
  162.2 1.4 dynamic-update-slice.1
  163.6 1.3 dynamic-slice.2
  164.9 10.4 %all-reduce.1 = f32[4]{0:T(128)S(1)} all-reduce(f32[4]{0:T(128)S(1)} %dynamic-update-slice.1), channel_id=1, replica_groups=mesh['dp_0'=4,'dp_1'=4,'dp_2'=4,'dp_3'=2,'mp'=4] {'dp_1'}, use_global_device_ids=true, to_apply=%add.1 | all-reduce | flops 4 | bytes 32
  175.3 0.6 reduce_sum.66
  175.9 1.4 dynamic-update-slice.2
  177.3 1.3 dynamic-slice.3
  178.5 13.5 %all-reduce.2 = f32[4]{0:T(128)S(1)} all-reduce(f32[4]{0:T(128)S(1)} %dynamic-update-slice.2), channel_id=1, replica_groups=mesh['dp_0'=4,'dp_1'=4,'dp_2'=4,'dp_3'=2,'mp'=4] {'dp_2'}, use_global_device_ids=true, to_apply=%add.2 | all-reduce | flops 4 | bytes 32
  192.0 0.6 reduce_sum.67
  192.6 1.4 dynamic-update-slice.3
  194.0 1.3 dynamic-slice.4
  195.3 2.4 %all-reduce.3 = f32[2]{0:T(128)S(1)} all-reduce(f32[2]{0:T(128)S(1)} %dynamic-update-slice.3), channel_id=1, replica_groups=mesh['dp_0'=4,'dp_1'=4,'dp_2'=4,'dp_3'=2,'mp'=4] {'dp_3'}, use_global_device_ids=true, to_apply=%add.3 | all-reduce | flops 2 | bytes 16
  197.7 0.6 reduce_sum.68
  198.3 1.4 dynamic-update-slice.4
  199.7 11.6 %all-reduce.4 = f32[4]{0:T(128)S(1)} all-reduce(f32[4]{0:T(128)S(1)} %dynamic-update-slice.4), channel_id=1, replica_groups=mesh['dp_0'=4,'dp_1'=4,'dp_2'=4,'dp_3'=2,'mp'=4] {'mp'}, use_global_device_ids=true, to_apply=%add.4 | all-reduce | flops 4 | bytes 32
  211.3 0.6 reduce_sum.69
  212.6 2.0 multiply_multiply_fusion
  (10 shorter events, 0.1 us)
Async XLA Ops:
  7.2 126.4 %all-gather.3.cloned.1.call-start = ((), (), s32[]{:S(2)}) async-start(), calls=%async_computation.4 | async-start | bytes 4227072 | tf_op jit(solution)/shard_map/all_gather | solution.py:55
  10.0 13.3 %all-to-all-start.1 = ((bf16[4,4,2048]{2,1,0:T(4,128)(2,1)}), bf16[4,4,2048]{2,1,0:T(4,128)(2,1)S(1)}, u32[]{:S(2)}, u32[]{:S(2)}) async-start(bf16[4,4,2048]{2,1,0:T(4,128)(2,1)} %broadcast_in_dim.2), calls=%async_computation.1 | async-start | bytes 131072 | tf_op jit(solution)/shard_map/all_to_all | solution.py:23
  27.7 34.7 %all-to-all-start = ((bf16[128,2,128]{2,1,0:T(2,128)(2,1)}), bf16[128,2,128]{2,1,0:T(2,128)(2,1)S(1)}, u32[]{:S(2)}, u32[]{:S(2)}) async-start(bf16[128,2,128]{2,1,0:T(2,128)(2,1)} %reshape.45), calls=%async_computation | async-start | bytes 131072 | tf_op jit(solution)/shard_map/all_to_all | solution.py:92
  62.4 23.5 %all-to-all-start.3 = ((bf16[64,2,256]{2,1,0:T(2,128)(2,1)}), bf16[64,2,256]{2,1,0:T(2,128)(2,1)S(1)}, u32[]{:S(2)}, u32[]{:S(2)}) async-start(bf16[64,2,256]{2,1,0:T(2,128)(2,1)} %reshape.49), calls=%async_computation.3 | async-start | bytes 131072 | tf_op jit(solution)/shard_map/all_to_all | solution.py:39
  140.5 5.2 %copy-start = (bf16[512,4096]{1,0:T(8,128)(2,1)S(1)}, bf16[512,4096]{1,0:T(8,128)(2,1)}, u32[]{:S(2)}) copy-start(bf16[512,4096]{1,0:T(8,128)(2,1)} %reshape.34) | copy-start | bytes 12582916
Sparse Core Ops, SparseCore 0:
  13.0 120.5 all-gather.2
